TPU v7x, 32 devices: a whole 2x2x4 slice. The times are simulated.
32 devices in a mesh: bank: 8 (over z, core), zero: 4 (over y, x).
Axes of the slice: x: 2, y: 2, z: 4, core: 2. Of those that a mesh axis runs over, the one named last changes fastest.
Arguments:
- master_gate: float32 [64, 2048, 1408], P('bank', 'zero'), may hold values from -0.1875 to 0.1875
- master_up: float32 [64, 2048, 1408], P('bank', 'zero'), may hold values from -0.1875 to 0.1875
- master_down: float32 [64, 1408, 2048], P('bank', None, 'zero'), may hold values from -0.21875 to 0.21875
- router_weight: float32 [2048, 64], P('zero', 'bank'), may hold values from -0.125 to 0.125
- router_gain: float32 [2048], P('zero'), may hold values from 0.25 to 1.75
Outputs:
- final_gate: bfloat16 [64, 2048, 1408], P('bank', None, 'zero')
- final_up: bfloat16 [64, 2048, 1408], P('bank', None, 'zero')
- final_down: bfloat16 [64, 1408, 2048], P('bank', 'zero')
- scale_gate: float32 [64, 1408], P('bank', 'zero')
- scale_up: float32 [64, 1408], P('bank', 'zero')
- scale_down: float32 [64, 1408], P('bank', 'zero')
- serve_router: bfloat16 [2048, 64], replicated
All inputs are finite; a program needn't handle non-finite values. Where the computation divides by a largest or mean magnitude, that divisor is 1e-20 or more.
Results may differ from a plain program's by a relative error of at most 0.0013.
Values may be sent and summed in bfloat16 or wider, within the bound.
A program may use at most 192 MiB of HBM per device.

v0:
```python
import jax
import jax.numpy as jnp
from jax import lax
from jax.sharding import PartitionSpec as P

D_MODEL = 2048


def local(master_gate, master_up, master_down, router_weight, router_gain):
    total_gate, total_up, total_down = lax.psum(
        (
            jnp.sum(jnp.abs(master_gate), axis=1),
            jnp.sum(jnp.abs(master_up), axis=1),
            jnp.sum(jnp.abs(master_down), axis=2),
        ),
        "zero",
    )
    scale_gate = total_gate / D_MODEL
    scale_up = total_up / D_MODEL
    scale_down = total_down / D_MODEL
    narrow_gate, narrow_up, narrow_down = (
        (master_gate / jnp.expand_dims(scale_gate, 1)).astype(jnp.bfloat16),
        (master_up / jnp.expand_dims(scale_up, 1)).astype(jnp.bfloat16),
        (master_down / jnp.expand_dims(scale_down, 2)).astype(jnp.bfloat16),
    )
    final_gate, final_up = (
        lax.all_to_all(narrow_gate, "zero", split_axis=2, concat_axis=1, tiled=True),
        lax.all_to_all(narrow_up, "zero", split_axis=2, concat_axis=1, tiled=True),
    )
    final_down = lax.all_to_all(narrow_down, "zero", split_axis=1, concat_axis=2, tiled=True)
    scale_gate = lax.dynamic_slice_in_dim(
        scale_gate, lax.axis_index("zero") * final_gate.shape[2], final_gate.shape[2], axis=1
    )
    scale_up = lax.dynamic_slice_in_dim(
        scale_up, lax.axis_index("zero") * final_up.shape[2], final_up.shape[2], axis=1
    )
    scale_down = lax.dynamic_slice_in_dim(
        scale_down, lax.axis_index("zero") * final_down.shape[1], final_down.shape[1], axis=1
    )
    part_router = (router_weight * router_gain[:, None]).astype(jnp.bfloat16)
    row_router = lax.all_gather(part_router, "zero", axis=0, tiled=True)
    serve_router = lax.all_gather(row_router, "bank", axis=1, tiled=True)
    return (final_gate, final_up, final_down, scale_gate, scale_up, scale_down, serve_router)


def solution(mesh):
    placed = (
        P("bank", "zero", None),
        P("bank", "zero", None),
        P("bank", None, "zero"),
        P("zero", "bank"),
        P("zero"),
    )
    return jax.shard_map(
        local,
        mesh=mesh,
        in_specs=placed,
        out_specs=(
            P("bank", None, "zero"),
            P("bank", None, "zero"),
            P("bank", "zero", None),
            P("bank", "zero"),
            P("bank", "zero"),
            P("bank", "zero"),
            P(),
        ),
        check_vma=False,
    )
```

profile of v0, /device:TPU:0, one launch (start us, length us, event | category | flops | bytes accessed | tf_op | source)
XLA Modules:
  0.0 620.0 jit_solution(9753489696694195745)
XLA Ops:
  7.2 0.0 all-reduce.3.cloned.1.call-start
  7.2 0.0 copy-start
  7.2 9.0 %abs_reduce_fusion = f32[8,1408]{1,0:T(8,128)} fusion(f32[8,1408,512]{2,1,0:T(8,128)} %param.7), kind=kLoop, calls=%fused_computation.2 | loop fusion | flops 11523072 | bytes 23113728 | tf_op jit(solution)/shard_map/reduce_sum | solution.py:14
  16.2 5.2 copy-done
  21.4 10.8 %abs_reduce_fusion.1 = (f32[8,1408]{1,0:T(8,128)}, f32[8,1408]{1,0:T(8,128)}) fusion(f32[8,512,1408]{2,1,0:T(8,128)S(1)} %copy-done, f32[8,512,1408]{2,1,0:T(8,128)} %param.5), kind=kLoop, calls=%fused_computation.4 | loop fusion | flops 23046144 | bytes 46227456 | tf_op jit(solution)/shard_map/reduce_sum | solution.py:13
  32.2 0.0 all-reduce.3.cloned.1.call-update
  32.2 23.7 %copy.28 = f32[8,512,1408]{1,0,2:T(8,128)} copy(f32[8,512,1408]{2,1,0:T(8,128)} %param.6) | data formatting | bytes 46137344 | tf_op args[1]
  55.9 21.4 %all-reduce.3.cloned.1.call-done = (f32[8,1408]{1,0:T(8,128)}, f32[8,1408]{1,0:T(8,128)}, f32[8,1408]{1,0:T(8,128)}) async-done(((f32[8,1408]{1,0:T(8,128)}, f32[8,1408]{1,0:T(8,128)}, f32[8,1408]{1,0:T(8,128)}), (f32[8,1408]{1,0:T(8,128)}, f32[8,1408]{1,0:T(8,128)}, f32[8,1408]{1,0:T(8,128)})) %all-reduce.3.cloned.1.call-update) | async-done | bytes 135184 | tf_op jit(solution)/shard_map/psum | solution.py:10
  77.3 0.8 broadcast_multiply_fusion.1
  78.1 0.3 copy.27
  78.4 13.3 %divide_convert_fusion = bf16[8,512,1408]{1,0,2:T(8,128)(2,1)} fusion(f32[8,512,1408]{1,0,2:T(8,128)} %copy.28, f32[8,1408]{0,1:T(8,128)S(1)} %copy.27), kind=kLoop, calls=%fused_computation.3 | loop fusion | flops 11534336 | bytes 34648064 | tf_op jit(solution)/shard_map/convert_element_type | solution.py:23
  91.7 6.2 %all-to-all-start.1 = ((bf16[8,512,1408]{1,0,2:T(8,128)(2,1)}), bf16[8,512,1408]{1,0,2:T(8,128)(2,1)}, u32[]{:S(2)}, u32[]{:S(2)}) async-start(bf16[8,512,1408]{1,0,2:T(8,128)(2,1)} %divide_convert_fusion), calls=%async_computation.1 | async-start | bytes 23068672 | tf_op jit(solution)/shard_map/all_to_all | solution.py:28
  97.9 0.0 copy-start.2
  98.0 23.7 %copy.24 = f32[8,512,1408]{1,0,2:T(8,128)} copy(f32[8,512,1408]{2,1,0:T(8,128)} %param.5) | data formatting | bytes 46137344 | tf_op args[0]
  121.6 0.0 copy-done.2
  121.6 0.3 copy.23
  121.9 0.0 copy-start.1
  121.9 13.3 %divide_convert_fusion.1 = bf16[8,512,1408]{1,0,2:T(8,128)(2,1)} fusion(f32[8,512,1408]{1,0,2:T(8,128)} %copy.24, f32[8,1408]{0,1:T(8,128)S(1)} %copy.23), kind=kLoop, calls=%fused_computation.5 | loop fusion | flops 11534336 | bytes 34648064 | tf_op jit(solution)/shard_map/convert_element_type | solution.py:22
  135.2 88.5 %all-to-all-done.1 = bf16[8,512,1408]{1,0,2:T(8,128)(2,1)} async-done(((bf16[8,512,1408]{1,0,2:T(8,128)(2,1)}), bf16[8,512,1408]{1,0,2:T(8,128)(2,1)}, u32[]{:S(2)}, u32[]{:S(2)}) %all-to-all-start.1) | async-done | bytes 11534368 | tf_op jit(solution)/shard_map/all_to_all | solution.py:28
  223.7 6.2 all-to-all-start
  229.9 0.0 copy-done.1
  229.9 0.3 copy.31
  230.2 0.0 copy-start.3
  230.2 0.0 copy-start.4
  230.2 29.5 %fusion = bf16[8,1408,512]{2,0,1:T(8,128)(2,1)} fusion(f32[8,1408,512]{2,1,0:T(8,128)} %param.7, f32[8,1408]{0,1:T(8,128)S(1)} %copy.31), kind=kLoop, calls=%fused_computation.1 | loop fusion | flops 11534336 | bytes 34648064 | tf_op jit(solution)/shard_map/convert_element_type | solution.py:24
  259.7 95.7 %all-to-all-done = bf16[8,512,1408]{1,0,2:T(8,128)(2,1)} async-done(((bf16[8,512,1408]{1,0,2:T(8,128)(2,1)}), bf16[8,512,1408]{1,0,2:T(8,128)(2,1)}, u32[]{:S(2)}, u32[]{:S(2)}) %all-to-all-start) | async-done | bytes 11534368 | tf_op jit(solution)/shard_map/all_to_all | solution.py:27
  355.4 6.2 %all-to-all-start.2 = ((bf16[8,1408,512]{2,0,1:T(8,128)(2,1)}), bf16[8,1408,512]{2,0,1:T(8,128)(2,1)}, u32[]{:S(2)}, u32[]{:S(2)}) async-start(bf16[8,1408,512]{2,0,1:T(8,128)(2,1)} %fusion), calls=%async_computation.2 | async-start | bytes 23068672 | tf_op jit(solution)/shard_map/all_to_all | solution.py:30
  361.7 0.0 copy-done.3
  361.7 0.0 copy-done.4
  361.7 128.8 %all_gather.6 = bf16[2048,8]{0,1:T(8,128)(2,1)S(1)} all-gather(bf16[512,8]{0,1:T(8,128)(2,1)S(1)} %multiply_convert_fusion), channel_id=1, replica_groups=mesh['bank'=8,'zero'=4] {'zero'}, dimensions={0}, use_global_device_ids=true | all-gather | bytes 40960 | tf_op jit(solution)/shard_map/all_gather | solution.py:41
  490.6 14.4 %all_gather.7 = bf16[2048,64]{0,1:T(8,128)(2,1)S(1)} all-gather(bf16[2048,8]{0,1:T(8,128)(2,1)S(1)} %all_gather.6), channel_id=1, replica_groups=mesh['bank'=8,'zero'=4] {'bank'}, dimensions={1}, use_global_device_ids=true | all-gather | bytes 294912 | tf_op jit(solution)/shard_map/all_gather | solution.py:42
  505.0 0.7 constant_dynamic-slice_fusion
  505.6 0.7 constant_dynamic-slice_fusion.1
  506.3 0.7 constant_dynamic-slice_fusion.2
  507.0 15.9 %copy.30 = bf16[8,4,512,352]{2,1,3,0:T(4,128)(2,1)} copy(bf16[8,4,512,352]{2,0,3,1:T(8,128)(2,1)} %bitcast.5) | data formatting | bytes 23068672 | tf_op jit(solution)/shard_map/all_to_all | solution.py:28
  522.9 19.3 %all_to_all.46 = bf16[8,2048,352]{1,2,0:T(8,128)(2,1)} reshape(bf16[8,4,512,352]{2,1,3,0:T(4,128)(2,1)} %copy.30) | data formatting | bytes 23068672 | tf_op jit(solution)/shard_map/all_to_all | solution.py:28
  542.1 15.9 %copy.26 = bf16[8,4,512,352]{2,1,3,0:T(4,128)(2,1)} copy(bf16[8,4,512,352]{2,0,3,1:T(8,128)(2,1)} %bitcast.2) | data formatting | bytes 23068672 | tf_op jit(solution)/shard_map/all_to_all | solution.py:27
  558.0 19.3 %all_to_all.42 = bf16[8,2048,352]{1,2,0:T(8,128)(2,1)} reshape(bf16[8,4,512,352]{2,1,3,0:T(4,128)(2,1)} %copy.26) | data formatting | bytes 23068672 | tf_op jit(solution)/shard_map/all_to_all | solution.py:27
  577.3 0.0 all-to-all-done.2
  577.3 15.9 %copy.33 = bf16[8,352,4,512]{3,2,1,0:T(4,128)(2,1)} copy(bf16[8,352,4,512]{3,0,1,2:T(8,128)(2,1)} %bitcast.7) | data formatting | bytes 23068672 | tf_op jit(solution)/shard_map/all_to_all | solution.py:30
  593.2 19.3 %all_to_all.50 = bf16[8,352,2048]{2,1,0:T(8,128)(2,1)} reshape(bf16[8,352,4,512]{3,2,1,0:T(4,128)(2,1)} %copy.33) | data formatting | bytes 23068672 | tf_op jit(solution)/shard_map/all_to_all | solution.py:30
  612.5 0.7 copy.43
  (3 shorter events, 0.0 us)
Async XLA Ops:
  7.2 70.2 %all-reduce.3.cloned.1.call-start = ((), (), s32[]{:S(2)}) async-start(), calls=%async_computation.3 | async-start | bytes 270336 | tf_op jit(solution)/shard_map/psum | solution.py:10
  7.2 14.2 %copy-start = (f32[8,512,1408]{2,1,0:T(8,128)S(1)}, f32[8,512,1408]{2,1,0:T(8,128)}, u32[]{:S(2)}) copy-start(f32[8,512,1408]{2,1,0:T(8,128)} %param.6) | copy-start | bytes 69206016
  91.7 132.0 %all-to-all-start.1 = ((bf16[8,512,1408]{1,0,2:T(8,128)(2,1)}), bf16[8,512,1408]{1,0,2:T(8,128)(2,1)}, u32[]{:S(2)}, u32[]{:S(2)}) async-start(bf16[8,512,1408]{1,0,2:T(8,128)(2,1)} %divide_convert_fusion), calls=%async_computation.1 | async-start | bytes 23068672 | tf_op jit(solution)/shard_map/all_to_all | solution.py:28
  97.9 23.7 %copy-start.2 = (f32[8,1408]{1,0:T(8,128)S(1)}, f32[8,1408]{1,0:T(8,128)}, u32[]{:S(2)}) copy-start(f32[8,1408]{1,0:T(8,128)} %get-tuple-element.7) | copy-start | bytes 135172
  121.9 108.0 %copy-start.1 = (f32[8,1408]{1,0:T(8,128)S(1)}, f32[8,1408]{1,0:T(8,128)}, u32[]{:S(2)}) copy-start(f32[8,1408]{1,0:T(8,128)} %get-tuple-element.9) | copy-start | bytes 135172
  223.7 131.7 %all-to-all-start = ((bf16[8,512,1408]{1,0,2:T(8,128)(2,1)}), bf16[8,512,1408]{1,0,2:T(8,128)(2,1)}, u32[]{:S(2)}, u32[]{:S(2)}) async-start(bf16[8,512,1408]{1,0,2:T(8,128)(2,1)} %divide_convert_fusion.1), calls=%async_computation | async-start | bytes 23068672 | tf_op jit(solution)/shard_map/all_to_all | solution.py:27
  230.2 131.5 %copy-start.3 = (f32[512,8]{0,1:T(8,128)S(1)}, f32[512,8]{0,1:T(8,128)}, u32[]{:S(2)}) copy-start(f32[512,8]{0,1:T(8,128)} %param.8) | copy-start | bytes 49156
  230.2 131.5 %copy-start.4 = (f32[512]{0:T(512)S(1)}, f32[512]{0:T(512)}, u32[]{:S(2)}) copy-start(f32[512]{0:T(512)} %param.9) | copy-start | bytes 6148
  355.4 221.8 %all-to-all-start.2 = ((bf16[8,1408,512]{2,0,1:T(8,128)(2,1)}), bf16[8,1408,512]{2,0,1:T(8,128)(2,1)}, u32[]{:S(2)}, u32[]{:S(2)}) async-start(bf16[8,1408,512]{2,0,1:T(8,128)(2,1)} %fusion), calls=%async_computation.2 | async-start | bytes 23068672 | tf_op jit(solution)/shard_map/all_to_all | solution.py:30
Sparse Core Ops, SparseCore 0:
  32.3 44.9 all-reduce.2
where the time goes:
time: 623 us; the launch traced here: 620 us
  waiting for transfers between devices  206 us (33%)
  local copies, waits for them, and re-layouts  162 us (26%)
  blocking collectives  143 us (23%)
  other arithmetic  76.7 us (12%)
  starting transfers between devices  18.6 us (3%)
  between operations  14.2 us (2%)
    all_gather x1, blocking collectives, local(): row_router = lax.all_gather(part_router, 'zero', axis=0, tiled=True)  129 us
    all_to_all x1, waiting for transfers between devices, local(): lax.all_to_all(narrow_gate, 'zero', split_axis=2, concat_axis=1, tiled=True)  95.7 us
    all_to_all x1, waiting for transfers between devices, local(): lax.all_to_all(narrow_up, 'zero', split_axis=2, concat_axis=1, tiled=True)  88.5 us
    unnamed x13, local copies, waits for them, and re-layouts  53.3 us
    all_to_all x2, local copies, waits for them, and re-layouts, local(): lax.all_to_all(narrow_down, 'zero', split_axis=1, concat_axis=2, tiled=True)  35.2 us
    all_to_all x2, local copies, waits for them, and re-layouts, local(): lax.all_to_all(narrow_up, 'zero', split_axis=2, concat_axis=1, tiled=True)  35.1 us
    all_to_all x2, local copies, waits for them, and re-layouts, local(): lax.all_to_all(narrow_gate, 'zero', split_axis=2, concat_axis=1, tiled=True)  35.1 us
    convert_element_type x1, other arithmetic, local(): (master_down / jnp.expand_dims(scale_down, 2)).astype(jnp.bfloat16)  29.5 us
  transfers between devices with their start and end apart: 4, of which 3 were waited for; matrix products, arithmetic and copies ran while one was open for 20% of the time, Pallas kernels for 0%

commit v1 on v0

v1 whole, which is shorter than its diff:
```python
import jax
import jax.numpy as jnp
from jax import lax
from jax.sharding import PartitionSpec as P


def exchange(wide, scale, parts):
    experts, rows, width = wide.shape
    narrow = (wide / scale[:, :, None]).astype(jnp.bfloat16)
    cut = narrow.reshape(experts, parts, rows // parts, width).transpose(1, 0, 2, 3)
    return lax.all_to_all(cut, "zero", split_axis=0, concat_axis=0, tiled=True), cut


def merged(blocks):
    return jnp.concatenate([blocks[p] for p in range(blocks.shape[0])], axis=2)


def local(parts, master_gate, master_up, master_down, router_weight, router_gain):
    experts, rows, inner = master_gate.shape
    d_model = rows * parts
    sums = jnp.stack(
        [
            jnp.sum(jnp.abs(master_gate), axis=1),
            jnp.sum(jnp.abs(master_up), axis=1),
            jnp.sum(jnp.abs(master_down), axis=2),
        ]
    )
    part_router = (router_weight * router_gain[:, None]).astype(jnp.bfloat16).T
    router = lax.all_gather(part_router, ("bank", "zero"), axis=0, tiled=False)
    sums, router = lax.optimization_barrier((sums, router))
    every = lax.all_gather(sums, "zero", axis=0, tiled=False)
    scales = jnp.sum(every, axis=0) / d_model
    router = router.reshape(-1, parts, experts, rows).transpose(0, 2, 1, 3)
    serve_router = router.reshape(-1, d_model).T

    got_down, cut = exchange(master_down, scales[2], parts)
    master_gate, cut = lax.optimization_barrier((master_gate, cut))
    got_gate, cut = exchange(master_gate.transpose(0, 2, 1), scales[0], parts)
    master_up, cut = lax.optimization_barrier((master_up, cut))
    got_up, cut = exchange(master_up.transpose(0, 2, 1), scales[1], parts)

    final_down = merged(got_down)
    final_gate = merged(got_gate).transpose(0, 2, 1)
    final_up = merged(got_up).transpose(0, 2, 1)
    own = lax.dynamic_slice_in_dim(
        scales, lax.axis_index("zero") * (inner // parts), inner // parts, axis=2
    )
    return (final_gate, final_up, final_down, own[0], own[1], own[2], serve_router)


def solution(mesh):
    placed = (
        P("bank", "zero", None),
        P("bank", "zero", None),
        P("bank", None, "zero"),
        P("zero", "bank"),
        P("zero"),
    )
    parts = mesh.shape["zero"]
    return jax.shard_map(
        lambda *arrays: local(parts, *arrays),
        mesh=mesh,
        in_specs=placed,
        out_specs=(
            P("bank", None, "zero"),
            P("bank", None, "zero"),
            P("bank", "zero", None),
            P("bank", "zero"),
            P("bank", "zero"),
            P("bank", "zero"),
            P(),
        ),
        check_vma=False,
    )
```

time: 623 us -> 524 us (0.84)
  local copies, waits for them, and re-layouts: 162 us -> 77.9 us
  waiting for transfers between devices: 206 us -> 276 us
  blocking collectives: 143 us -> 79.7 us
  between operations: 14.2 us -> 0.89 us
  other arithmetic: 76.7 us -> 69.2 us
    all_to_all x6 -> x0, local copies, waits for them, and re-layouts: 105 us -> none  [the longest x2 35.2 us: local(): lax.all_to_all(narrow_down, 'zero', split_axis=1, concat_axis=2, tiled=True)]
    all_to_all x3, waiting for transfers between devices: 184 us -> 276 us  [exchange(): lax.all_to_all(cut, 'zero', split_axis=0, concat_axis=0, tiled=True)]
    all_gather x2, blocking collectives: 143 us -> 79.7 us  [the longest x1 71.1 us: local(): router = lax.all_gather(part_router, ('bank', 'zero'), axis=0, tiled=False)]
    unnamed x13 -> x17, local copies, waits for them, and re-layouts: 53.3 us -> 0.75 us
    optimization_barrier x0 -> x2, local copies, waits for them, and re-layouts: none -> 46.8 us  [the longest x1 23.4 us: local(): master_gate, cut = lax.optimization_barrier((master_gate, cut))]
    convert_element_type x4 -> x3, other arithmetic: 56.2 us -> 28.3 us  [exchange(): narrow = (wide / scale[:, :, None]).astype(jnp.bfloat16)]
    psum x1 -> x0, waiting for transfers between devices: 21.4 us -> none  [local(): lax.psum((jnp.sum(jnp.abs(master_gate), axis=1), jnp.sum(jnp.abs(master_u...]
    squeeze x0 -> x4, local copies, waits for them, and re-layouts: none -> 15.3 us  [the longest x3 14.6 us: merged(): return jnp.concatenate([blocks[p] for p in range(blocks.shape[0])], axis=2)]
  transfers between devices with their start and end apart: 4 -> 3, of which waited for: 3 -> 3; matrix products, arithmetic and copies ran while one was open for 20% -> 18% of each run, Pallas kernels for 0% -> 0%
where the time goes in v1:
time: 524 us; the launch traced here: 523 us
  waiting for transfers between devices  276 us (53%)
  blocking collectives  79.7 us (15%)
  local copies, waits for them, and re-layouts  77.9 us (15%)
  other arithmetic  69.2 us (13%)
  starting transfers between devices  18.6 us (4%)
    all_to_all x3, waiting for transfers between devices, exchange(): lax.all_to_all(cut, 'zero', split_axis=0, concat_axis=0, tiled=True)  276 us
    all_gather x1, blocking collectives, local(): router = lax.all_gather(part_router, ('bank', 'zero'), axis=0, tiled=False)  71.1 us
    convert_element_type x3, other arithmetic, exchange(): narrow = (wide / scale[:, :, None]).astype(jnp.bfloat16)  28.3 us
    optimization_barrier x1, local copies, waits for them, and re-layouts, local(): master_gate, cut = lax.optimization_barrier((master_gate, cut))  23.4 us
    optimization_barrier x1, local copies, waits for them, and re-layouts, local(): master_up, cut = lax.optimization_barrier((master_up, cut))  23.4 us
    all_to_all x3, starting transfers between devices, exchange(): lax.all_to_all(cut, 'zero', split_axis=0, concat_axis=0, tiled=True)  18.6 us
    transpose x3, local copies, waits for them, and re-layouts, exchange(): narrow.reshape(experts, parts, rows // parts, width).transpose(1, 0, 2, 3)  15.1 us
    squeeze x3, local copies, waits for them, and re-layouts, merged(): return jnp.concatenate([blocks[p] for p in range(blocks.shape[0])], axis=2)  14.6 us
  transfers between devices with their start and end apart: 3, of which 3 were waited for; matrix products, arithmetic and copies ran while one was open for 18% of the time, Pallas kernels for 0%

profile of v1, /device:TPU:0, one launch (start us, length us, event | category | flops | bytes accessed | tf_op | source)
XLA Modules:
  0.0 522.6 jit_solution(1423111512351173173)
XLA Ops:
  0.6 0.0 slice-start
  0.6 0.0 slice-start.1
  0.7 0.0 slice-start.2
  0.7 10.4 %abs_reduce_fusion.2 = f32[8,1408]{1,0:T(8,128)S(1)} fusion(f32[8,512,1408]{2,1,0:T(8,128)} %param.5), kind=kLoop, calls=%fused_computation.5 | loop fusion | flops 11523072 | bytes 23113728 | tf_op jit(solution)/shard_map/reduce_sum | solution.py:23
  11.1 0.0 slice-start.3
  11.1 0.0 slice-start.4
  11.1 0.0 slice-start.5
  11.1 11.0 %abs_reduce_fusion.1 = f32[8,1408]{1,0:T(8,128)S(1)} fusion(f32[8,512,1408]{2,1,0:T(8,128)} %param.6), kind=kLoop, calls=%fused_computation.4 | loop fusion | flops 11523072 | bytes 23113728 | tf_op jit(solution)/shard_map/reduce_sum | solution.py:24
  22.1 0.0 slice-done
  22.1 0.0 slice-done.1
  22.1 0.0 slice-done.2
  22.1 0.0 slice-done.3
  22.1 0.0 slice-done.4
  22.1 0.0 slice-done.5
  22.1 0.0 copy-start
  22.1 0.0 copy-start.1
  22.2 3.9 abs_reduce_fusion
  26.1 0.0 copy-done
  26.1 0.0 copy-done.1
  26.1 71.1 %all-gather = bf16[256,512]{1,0:T(8,128)(2,1)S(1)} all-gather(bf16[8,512]{1,0:T(8,128)(2,1)S(1)} %fusion), channel_id=2, replica_groups=mesh['bank'=8,'zero'=4] {'bank','zero'}, dimensions={0}, use_global_device_ids=true | all-gather | bytes 270336 | tf_op jit(solution)/shard_map/all_gather | solution.py:29
  97.2 8.6 %all-gather.1 = f32[12,8,1408]{2,1,0:T(8,128)S(1)} all-gather(f32[3,8,1408]{2,1,0:T(8,128)S(1)} %pad_maximum_fusion.1), channel_id=3, replica_groups=mesh['bank'=8,'zero'=4] {'zero'}, dimensions={0}, use_global_device_ids=true | all-gather | bytes 675840 | tf_op jit(solution)/shard_map/all_gather | solution.py:31
  105.9 9.4 %divide_convert_fusion.2 = bf16[8,1408,512]{2,1,0:T(8,128)(2,1)S(1)} fusion(f32[8,1408,512]{2,1,0:T(8,128)} %param.7, f32[8,1408]{1,0:T(8,128)S(1)} %get-tuple-element.32), kind=kLoop, calls=%fused_computation.2 | loop fusion | flops 11534336 | bytes 34648064 | tf_op jit(solution)/shard_map/convert_element_type | solution.py:9
  115.4 5.0 copy.27
  120.4 6.2 %all-to-all-start.2 = ((bf16[4,8,352,512]{3,2,1,0:T(8,128)(2,1)}), bf16[4,8,352,512]{3,2,1,0:T(8,128)(2,1)}, u32[]{:S(2)}, u32[]{:S(2)}) async-start(bf16[4,8,352,512]{3,2,1,0:T(8,128)(2,1)} %copy.27), calls=%async_computation.2 | async-start | bytes 23068672 | tf_op jit(solution)/shard_map/all_to_all | solution.py:11
  126.6 23.4 %copy.23 = f32[8,512,1408]{1,2,0:T(8,128)} copy(f32[8,512,1408]{2,1,0:T(8,128)} %param.5) | data formatting | bytes 46137344 | tf_op jit(solution)/shard_map/optimization_barrier | solution.py:37
  150.0 9.4 %divide_convert_fusion.1 = bf16[8,512,1408]{1,2,0:T(8,128)(2,1)S(1)} fusion(f32[8,512,1408]{1,2,0:T(8,128)} %copy.23, f32[8,1408]{1,0:T(8,128)S(1)} %get-tuple-element.31), kind=kLoop, calls=%fused_computation.1 | loop fusion | flops 11534336 | bytes 34648064 | tf_op jit(solution)/shard_map/convert_element_type | solution.py:9
  159.4 5.0 copy.24
  164.4 82.9 %all-to-all-done.2 = bf16[4,8,352,512]{3,2,1,0:T(8,128)(2,1)} async-done(((bf16[4,8,352,512]{3,2,1,0:T(8,128)(2,1)}), bf16[4,8,352,512]{3,2,1,0:T(8,128)(2,1)}, u32[]{:S(2)}, u32[]{:S(2)}) %all-to-all-start.2) | async-done | bytes 11534368 | tf_op jit(solution)/shard_map/all_to_all | solution.py:11
  247.4 6.2 %all-to-all-start = ((bf16[4,8,352,512]{3,2,1,0:T(8,128)(2,1)}), bf16[4,8,352,512]{3,2,1,0:T(8,128)(2,1)}, u32[]{:S(2)}, u32[]{:S(2)}) async-start(bf16[4,8,352,512]{3,2,1,0:T(8,128)(2,1)} %copy.24), calls=%async_computation | async-start | bytes 23068672 | tf_op jit(solution)/shard_map/all_to_all | solution.py:11
  253.6 23.4 %copy.25 = f32[8,512,1408]{1,2,0:T(8,128)} copy(f32[8,512,1408]{2,1,0:T(8,128)} %param.6) | data formatting | bytes 46137344 | tf_op jit(solution)/shard_map/optimization_barrier | solution.py:39
  277.0 9.4 %divide_convert_fusion = bf16[8,512,1408]{1,2,0:T(8,128)(2,1)S(1)} fusion(f32[8,512,1408]{1,2,0:T(8,128)} %copy.25, f32[8,1408]{1,0:T(8,128)S(1)} %get-tuple-element.30), kind=kLoop, calls=%fused_computation | loop fusion | flops 11534336 | bytes 34648064 | tf_op jit(solution)/shard_map/convert_element_type | solution.py:9
  286.4 5.0 copy.26
  291.5 88.6 %all-to-all-done = bf16[4,8,352,512]{3,2,1,0:T(8,128)(2,1)} async-done(((bf16[4,8,352,512]{3,2,1,0:T(8,128)(2,1)}), bf16[4,8,352,512]{3,2,1,0:T(8,128)(2,1)}, u32[]{:S(2)}, u32[]{:S(2)}) %all-to-all-start) | async-done | bytes 11534368 | tf_op jit(solution)/shard_map/all_to_all | solution.py:11
  380.0 6.2 %all-to-all-start.1 = ((bf16[4,8,352,512]{3,2,1,0:T(8,128)(2,1)}), bf16[4,8,352,512]{3,2,1,0:T(8,128)(2,1)}, u32[]{:S(2)}, u32[]{:S(2)}) async-start(bf16[4,8,352,512]{3,2,1,0:T(8,128)(2,1)} %copy.26), calls=%async_computation.1 | async-start | bytes 23068672 | tf_op jit(solution)/shard_map/all_to_all | solution.py:11
  386.2 0.7 dynamic-slice_bitcast_fusion
  386.9 4.9 slice_bitcast_fusion.3
  391.8 4.9 slice_bitcast_fusion.11
  396.7 5.2 pad_maximum_fusion
  401.9 5.2 maximum_bitcast_fusion
  407.1 104.8 %all-to-all-done.1 = bf16[4,8,352,512]{3,2,1,0:T(8,128)(2,1)} async-done(((bf16[4,8,352,512]{3,2,1,0:T(8,128)(2,1)}), bf16[4,8,352,512]{3,2,1,0:T(8,128)(2,1)}, u32[]{:S(2)}, u32[]{:S(2)}) %all-to-all-start.1) | async-done | bytes 11534368 | tf_op jit(solution)/shard_map/all_to_all | solution.py:11
  511.9 4.9 slice_bitcast_fusion.7
  516.7 5.2 maximum_bitcast_fusion.1
  521.9 0.7 copy.29
  (6 shorter events, 0.1 us)
Async XLA Ops:
  0.6 21.4 %slice-start = ((s8[23068672]{0:T(1024)(128)(4,1)}), s8[4194304]{0:T(1024)(128)(4,1)S(1)}, s32[]{:S(2)}) async-start(s8[23068672]{0:T(1024)(128)(4,1)} %bitcast.67), calls=%async_computation.3 | async-start | bytes 8388608
  0.6 21.4 %slice-start.1 = ((s8[23068672]{0:T(1024)(128)(4,1)}), s8[4194304]{0:T(1024)(128)(4,1)S(1)}, s32[]{:S(2)}) async-start(s8[23068672]{0:T(1024)(128)(4,1)} %bitcast.67), calls=%async_computation.4 | async-start | bytes 8388608
  0.7 21.4 %slice-start.2 = ((s8[23068672]{0:T(1024)(128)(4,1)}), s8[4194304]{0:T(1024)(128)(4,1)S(1)}, s32[]{:S(2)}) async-start(s8[23068672]{0:T(1024)(128)(4,1)} %bitcast.67), calls=%async_computation.5 | async-start | bytes 8388608
  11.1 11.0 %slice-start.3 = ((s8[23068672]{0:T(1024)(128)(4,1)}), s8[4194304]{0:T(1024)(128)(4,1)S(1)}, s32[]{:S(2)}) async-start(s8[23068672]{0:T(1024)(128)(4,1)} %bitcast.67), calls=%async_computation.6 | async-start | bytes 8388608
  11.1 11.0 %slice-start.4 = ((s8[23068672]{0:T(1024)(128)(4,1)}), s8[4194304]{0:T(1024)(128)(4,1)S(1)}, s32[]{:S(2)}) async-start(s8[23068672]{0:T(1024)(128)(4,1)} %bitcast.67), calls=%async_computation.7 | async-start | bytes 8388608
  11.1 11.0 %slice-start.5 = ((s8[23068672]{0:T(1024)(128)(4,1)}), s8[2097152]{0:T(1024)(128)(4,1)S(1)}, s32[]{:S(2)}) async-start(s8[23068672]{0:T(1024)(128)(4,1)} %bitcast.67), calls=%async_computation.8 | async-start | bytes 4194304
  22.1 4.0 copy-start
  22.1 4.0 copy-start.1
  120.4 127.0 %all-to-all-start.2 = ((bf16[4,8,352,512]{3,2,1,0:T(8,128)(2,1)}), bf16[4,8,352,512]{3,2,1,0:T(8,128)(2,1)}, u32[]{:S(2)}, u32[]{:S(2)}) async-start(bf16[4,8,352,512]{3,2,1,0:T(8,128)(2,1)} %copy.27), calls=%async_computation.2 | async-start | bytes 23068672 | tf_op jit(solution)/shard_map/all_to_all | solution.py:11
  247.4 132.7 %all-to-all-start = ((bf16[4,8,352,512]{3,2,1,0:T(8,128)(2,1)}), bf16[4,8,352,512]{3,2,1,0:T(8,128)(2,1)}, u32[]{:S(2)}, u32[]{:S(2)}) async-start(bf16[4,8,352,512]{3,2,1,0:T(8,128)(2,1)} %copy.24), calls=%async_computation | async-start | bytes 23068672 | tf_op jit(solution)/shard_map/all_to_all | solution.py:11
  380.0 131.8 %all-to-all-start.1 = ((bf16[4,8,352,512]{3,2,1,0:T(8,128)(2,1)}), bf16[4,8,352,512]{3,2,1,0:T(8,128)(2,1)}, u32[]{:S(2)}, u32[]{:S(2)}) async-start(bf16[4,8,352,512]{3,2,1,0:T(8,128)(2,1)} %copy.26), calls=%async_computation.1 | async-start | bytes 23068672 | tf_op jit(solution)/shard_map/all_to_all | solution.py:11
